TPU v7x, 128 devices: a whole 4x4x4 slice. The times are simulated.
128 devices in a mesh: gx: 2 (over core), gy: 64 (over z, y, x).
Axes of the slice: x: 4, y: 4, z: 4, core: 2. Of those that a mesh axis runs over, the one named last changes fastest.
Arguments:
- right_side: float32 [128, 16384], P('gx', 'gy'), may hold values from -34 to 34, as said below
- initial: float32 [128, 16384], P('gx', 'gy'), may hold values from -0.6 to 0.6
- reaction: float32 [128, 16384], P('gx', 'gy'), may hold values from 0.05 to 0.5
- velocity_x: float32 [128, 16384], P('gx', 'gy'), may hold values from -1 to 1
- velocity_y: float32 [128, 16384], P('gx', 'gy'), may hold values from -1 to 1
Outputs:
- solution: float32 [128, 16384], P('gx', 'gy')
- residual: float32 [128, 16384], P('gx', 'gy')
Inputs may be any that keep to these rules, and one draw needn't show every extreme that they name: right_side is noise bounded by 4 in size times an envelope 0.5 + 8 g, where g is a periodic Gaussian bump of one device block's width along each dimension centred at a drawn position, so its entries lie within -34 and 34.
All inputs are finite; a program needn't handle non-finite values.
Results may differ from a plain program's by a relative error of at most 0.0075.
Values sent between devices are 32-bit elements.
A program may use at most 64 MiB of HBM per device.

v0:
```python
import jax
import jax.numpy as jnp
from jax import lax
from jax.sharding import Mesh
from jax.sharding import PartitionSpec as P

RESTART = 15
GX_GY = ("gx", "gy_0", "gy_1", "gy_2")
GY = ("gy_0", "gy_1", "gy_2")


def padded_2(cells, sides, width, closed):
    for axis, dim in sides:
        count = lax.axis_size(axis)
        ends = count if closed else count - 1
        head = lax.slice_in_dim(cells, 0, width, axis=dim)
        tail = lax.slice_in_dim(cells, cells.shape[dim] - width, cells.shape[dim], axis=dim)
        cells = jnp.concatenate(
            [
                lax.ppermute(tail, axis, [(i, (i + 1) % count) for i in range(ends)]),
                cells,
                lax.ppermute(head, axis, [((i + 1) % count, i) for i in range(ends)]),
            ],
            axis=dim,
        )
    return cells


def one_axis_at_a_time(x, axes):
    for axis in axes:
        x = lax.psum(x, axis)
    return x


def shifted(padded, offset, dimension, extent):
    row_start = 2 + offset if dimension == 0 else 2
    column_start = 2 + offset if dimension == 1 else 2
    return lax.slice(
        padded, (row_start, column_start), (row_start + extent[0], column_start + extent[1])
    )


def first_diff(padded, dimension, extent):
    outer = shifted(padded, -2, dimension, extent) - shifted(padded, 2, dimension, extent)
    inner = shifted(padded, 1, dimension, extent) - shifted(padded, -1, dimension, extent)
    return (outer + 8.0 * inner) / 12.0


def second_diff(padded, dimension, extent):
    inner = shifted(padded, 1, dimension, extent) + shifted(padded, -1, dimension, extent)
    outer = shifted(padded, 2, dimension, extent) + shifted(padded, -2, dimension, extent)
    return (16.0 * inner - outer - 30.0 * shifted(padded, 0, dimension, extent)) / 12.0


def apply_operator(field, padded_field, padded_speeds, reaction, velocity_x, velocity_y):
    extent = field.shape
    diffusion = second_diff(padded_field, 0, extent) + second_diff(padded_field, 1, extent)
    advect_x = 0.5 * (
        velocity_x * first_diff(padded_field, 0, extent)
        + first_diff(padded_speeds[0] * padded_field, 0, extent)
    )
    advect_y = 0.5 * (
        velocity_y * first_diff(padded_field, 1, extent)
        + first_diff(padded_speeds[1] * padded_field, 1, extent)
    )
    return reaction * field - diffusion + advect_x + advect_y


def least_squares(hessenberg, beta):
    columns_total = hessenberg.shape[1]
    target = jnp.where(jnp.arange(columns_total + 1) == 0, beta, 0.0)

    def rotate(column, carried):
        upper, target = carried
        top_row = upper[column]
        next_row = upper[column + 1]
        diagonal_entry = top_row[column]
        below_entry = next_row[column]
        radius = jnp.sqrt(diagonal_entry * diagonal_entry + below_entry * below_entry)
        cosine = diagonal_entry / radius
        sine_value = below_entry / radius
        upper = upper.at[column].set(cosine * top_row + sine_value * next_row)
        upper = upper.at[column + 1].set(cosine * next_row - sine_value * top_row)
        upper_value = target[column]
        lower_value = target[column + 1]
        target = target.at[column].set(cosine * upper_value + sine_value * lower_value)
        target = target.at[column + 1].set(cosine * lower_value - sine_value * upper_value)
        return (upper, target)

    upper, target = lax.fori_loop(0, columns_total, rotate, (hessenberg, target))

    def substitute(count, weights):
        row_index = columns_total - 1 - count
        known = jnp.sum(upper[row_index] * weights)
        return weights.at[row_index].set((target[row_index] - known) / upper[row_index, row_index])

    return lax.fori_loop(0, columns_total, substitute, jnp.zeros((columns_total,), jnp.float32))


def per_device(right_side, initial, reaction, velocity_x, velocity_y):
    row_count, column_count = right_side.shape
    speeds = jnp.stack([velocity_x, velocity_y])
    padded_speeds = padded_2(speeds, (("gx", 1), (GY, 2)), 2, True)

    def operator_on(field):
        padded_field = padded_2(field, (("gx", 0), (GY, 1)), 2, True)
        return apply_operator(field, padded_field, padded_speeds, reaction, velocity_x, velocity_y)

    start_residual = right_side - operator_on(initial)
    start_square = one_axis_at_a_time(jnp.sum(start_residual * start_residual), GX_GY)
    beta = jnp.sqrt(start_square)
    basis = jnp.zeros((RESTART + 1, row_count, column_count), jnp.float32)
    basis = basis.at[0].set(start_residual / beta)
    hessenberg = jnp.zeros((RESTART + 1, RESTART), jnp.float32)
    positions = jnp.arange(RESTART + 1)

    def arnoldi(column, carried):
        basis, hessenberg = carried
        current = lax.dynamic_index_in_dim(basis, column, 0, keepdims=False)
        applied = operator_on(current)
        local_projection = jnp.einsum("kxy,xy->k", basis, applied, precision=lax.Precision.HIGHEST)
        projection, applied_square = (
            one_axis_at_a_time(local_projection, GX_GY),
            one_axis_at_a_time(jnp.sum(applied * applied), GX_GY),
        )
        applied = applied - jnp.einsum(
            "k,kxy->xy", projection, basis, precision=lax.Precision.HIGHEST
        )
        length = jnp.sqrt(applied_square - jnp.sum(projection * projection))
        entries = jnp.where(positions == column + 1, length, projection)
        hessenberg = lax.dynamic_update_slice(hessenberg, entries[:, None], (0, column))
        basis = lax.dynamic_update_index_in_dim(basis, applied / length, column + 1, 0)
        return (basis, hessenberg)

    basis, hessenberg = lax.fori_loop(0, RESTART, arnoldi, (basis, hessenberg))
    weights = least_squares(hessenberg, beta)
    padded_weights = jnp.concatenate([weights, jnp.zeros((1,), jnp.float32)])
    solution = initial + jnp.einsum(
        "k,kxy->xy", padded_weights, basis, precision=lax.Precision.HIGHEST
    )
    leftover = jnp.where(positions == 0, beta, 0.0) - jnp.dot(
        hessenberg, weights, precision=lax.Precision.HIGHEST
    )
    residual = jnp.einsum("k,kxy->xy", leftover, basis, precision=lax.Precision.HIGHEST)
    return (solution, residual)


def solution(mesh):
    torus = Mesh(mesh.devices.reshape(mesh.shape["gx"], 4, 4, 4), ("gx", "gy_0", "gy_1", "gy_2"))
    placed = (P("gx", GY), P("gx", GY), P("gx", GY), P("gx", GY), P("gx", GY))
    return jax.shard_map(
        per_device,
        mesh=torus,
        in_specs=placed,
        out_specs=(P("gx", GY), P("gx", GY)),
        check_vma=False,
    )
```

profile of v0, /device:TPU:1, one launch (start us, length us, event | category | flops | bytes accessed | tf_op | source)
XLA Modules:
  0.0 1030.0 jit_solution(6680681950074222786)
XLA Ops:
  4.6 8.6 collective-permute-start.6
  13.4 7.0 collective-permute-start.11
  42.7 13.4 %psum.143 = f32[]{:T(128)} all-reduce(f32[]{:T(128)} %psum.142), channel_id=1, replica_groups=mesh['gx'=2,'gy_0'=4,'gy_1'=4,'gy_2'=4] {'gy_2'}, use_global_device_ids=true, to_apply=%region_4.0 | all-reduce | flops 1 | bytes 8 | tf_op jit(solution)/shard_map/psum | solution.py:31
  56.8 747.0 %while.56 = (s32[]{:T(128)}, f32[16,64,256]{2,1,0:T(8,128)S(1)}, f32[16,15]{0,1:T(8,128)S(1)}, f32[64,256]{1,0:T(8,128)S(1)}, f32[64,256]{1,0:T(8,128)S(1)}, /*i...) while((s32[]{:T(128)}, f32[16,64,256]{2,1,0:T(8,128)S(1)}, ...), condition=%wide.region_16.0_spmd.clone, body=%wide.region_5.16_spmd.clone.sunk | while | flops 7373337 | bytes 4410527 | solution.py:135
  79.9 6.7 all-reduce.10
  93.2 6.7 all-reduce.12
  115.5 7.2 collective-permute-done.3
  129.9 6.7 all-reduce.10
  143.2 6.8 all-reduce.12
  165.6 7.2 collective-permute-done.3
  180.0 6.7 all-reduce.10
  193.3 6.8 all-reduce.12
  215.6 7.2 collective-permute-done.3
  230.0 6.7 all-reduce.10
  243.3 6.8 all-reduce.12
  265.7 7.2 collective-permute-done.3
  280.1 6.7 all-reduce.10
  293.4 6.8 all-reduce.12
  315.7 7.2 collective-permute-done.3
  330.1 6.7 all-reduce.10
  343.4 6.8 all-reduce.12
  365.8 7.2 collective-permute-done.3
  380.2 6.7 all-reduce.10
  393.5 6.8 all-reduce.12
  415.8 7.2 collective-permute-done.3
  430.2 6.7 all-reduce.10
  443.5 6.8 all-reduce.12
  465.9 7.2 collective-permute-done.3
  480.3 6.7 all-reduce.10
  493.6 6.8 all-reduce.12
  515.9 7.2 collective-permute-done.3
  530.3 6.7 all-reduce.10
  543.6 6.8 all-reduce.12
  566.0 7.2 collective-permute-done.3
  580.4 6.7 all-reduce.10
  593.7 6.8 all-reduce.12
  616.0 7.2 collective-permute-done.3
  643.7 6.8 all-reduce.12
  666.1 7.2 collective-permute-done.3
  693.8 6.8 all-reduce.12
  716.1 7.2 collective-permute-done.3
  730.5 6.7 all-reduce.10
  743.8 6.8 all-reduce.12
  766.2 7.2 collective-permute-done.3
  780.6 6.7 all-reduce.10
  793.9 6.8 all-reduce.12
  804.5 162.3 %while.54 = (s32[]{:T(128)}, f32[16,15]{1,0:T(8,128)S(1)}, f32[16]{0:T(128)S(1)}, s32[]{:T(128)}, s32[2]{0:T(128)S(1)}, /*index=5*/s32[1]{0:T(128)}, s32[]{:T(128)}, s32[]{:T(128)}, s32[]{:T(128)}, s32[]{:T(128)}) while((s32[]{:T(128)}, f32[16,15]{1,0:T(8,128)S(1)}, f32[16]{0:T(128)S(1)}, s32[]{:T(128)}, s32[2]{0:T(128)S(1)}, ...), condition=%wide.region_20.21_spmd, body=%wide.region_17.20_spmd.sunk | while | flops 165 | bytes 5167 | solution.py:90
  966.8 59.4 %while.55 = (s32[]{:T(128)}, f32[15]{0:T(128)S(1)}, f32[16]{0:T(128)S(1)}, f32[16,15]{1,0:T(8,128)S(1)}, s32[]{:T(128)}, /*index=5*/s32[]{:T(128)}, s32[]{:T(128)}, s32[]{:T(128)}, s32[]{:T(128)}) while((s32[]{:T(128)}, f32[15]{0:T(128)S(1)}, f32[16]{0:T(128)S(1)}, f32[16,15]{1,0:T(8,128)S(1)}, s32[]{:T(128)}, /*index=5*/s32[]{:T(128)}, ...), condition=%wide.region_23.24_spmd, body=%wide.region_21.23_spmd.sunk | while | flops 43 | bytes 490 | solution.py:97
  (610 shorter events, 561.6 us)
Async XLA Ops:
  1.4 11.7 %collective-permute-start.8 = (f32[2,2,256]{2,1,0:T(2,128)S(1)}, f32[2,2,256]{2,1,0:T(2,128)S(1)}, u32[]{:S(2)}, u32[]{:S(2)}) collective-permute-start(f32[2,2,256]{2,1,0:T(2,128)S(1)} %get-tuple-element.581), channel_id=1, source_target_pairs={{0,64},{64,0},{1,65},{65,1},{2,66},{66,2},{3,67},{67,3},{4,68},{68... | collective-permute-start | bytes 12296 | tf_op jit(solution)/shard_map/ppermute | solution.py:20
  2.8 10.4 %collective-permute-start.9 = (f32[2,2,256]{2,1,0:T(2,128)S(1)}, f32[2,2,256]{2,1,0:T(2,128)S(1)}, u32[]{:S(2)}, u32[]{:S(2)}) collective-permute-start(f32[2,2,256]{2,1,0:T(2,128)S(1)} %get-tuple-element.582), channel_id=1, source_target_pairs={{64,0},{0,64},{65,1},{1,65},{66,2},{2,66},{67,3},{3,67},{68,4},{4,... | collective-permute-start | bytes 12296 | tf_op jit(solution)/shard_map/ppermute | solution.py:22
  4.6 15.7 %collective-permute-start.6 = (f32[68,2]{1,0:T(8,128)S(1)}, f32[68,2]{1,0:T(8,128)S(1)}, u32[]{:S(2)}, u32[]{:S(2)}) collective-permute-start(f32[68,2]{1,0:T(8,128)S(1)} %get-tuple-element.584), channel_id=1, source_target_pairs={{1,0},{2,1},{3,2},{4,3},{5,4},{6,5},{7,6},{8,7},{9,8},{10,9},{11,1... | collective-permute-start | bytes 1640 | tf_op jit(solution)/shard_map/ppermute | solution.py:22
  13.1 8.2 collective-permute-start.7
  13.3 9.4 collective-permute-start.10
  13.4 9.4 collective-permute-start.11
  56.9 7.3 collective-permute-start
  64.6 8.3 collective-permute-start.3
  103.2 7.3 collective-permute-start
  110.9 4.6 collective-permute-start.2
  114.5 8.2 collective-permute-start.3
  153.2 7.3 collective-permute-start
  161.0 4.6 collective-permute-start.2
  164.5 8.2 collective-permute-start.3
  203.3 7.3 collective-permute-start
  211.0 4.6 collective-permute-start.2
  214.6 8.2 collective-permute-start.3
  253.3 7.3 collective-permute-start
  264.6 8.2 collective-permute-start.3
  303.4 7.3 collective-permute-start
  314.7 8.2 collective-permute-start.3
  353.4 7.3 collective-permute-start
  361.2 4.6 collective-permute-start.2
  364.7 8.2 collective-permute-start.3
  403.5 7.3 collective-permute-start
  411.2 4.6 collective-permute-start.2
  414.8 8.2 collective-permute-start.3
  453.5 7.3 collective-permute-start
  461.3 4.6 collective-permute-start.2
  464.8 8.2 collective-permute-start.3
  503.6 7.3 collective-permute-start
  511.3 4.6 collective-permute-start.2
  514.9 8.2 collective-permute-start.3
  553.6 7.3 collective-permute-start
  561.4 4.6 collective-permute-start.2
  564.9 8.2 collective-permute-start.3
  603.7 7.3 collective-permute-start
  611.4 4.6 collective-permute-start.2
  615.0 8.2 collective-permute-start.3
  653.7 7.3 collective-permute-start
  661.5 4.6 collective-permute-start.2
  665.0 8.2 collective-permute-start.3
  703.8 7.3 collective-permute-start
  711.5 4.6 collective-permute-start.2
  715.1 8.2 collective-permute-start.3
  753.8 7.3 collective-permute-start
  761.6 4.6 collective-permute-start.2
  765.1 8.2 collective-permute-start.3
  (26 other events, 53.9 us)
where the time goes:
time: 1040 us; the launch traced here: 1030 us
  blocking collectives  398 us (38%)
  starting transfers between devices  167 us (16%)
  loops' own time  149 us (14%)
  waiting for transfers between devices  141 us (14%)
  other arithmetic  84.3 us (8%)
  matrix products  46.7 us (4%)
  local copies, waits for them, and re-layouts  42.3 us (4%)
    psum x64, blocking collectives, one_axis_at_a_time(): x = lax.psum(x, axis)  398 us
    ppermute x34, starting transfers between devices, padded_2(): lax.ppermute(head, axis, [((i + 1) % count, i) for i in range(ends)])  163 us
    ppermute x34, waiting for transfers between devices, padded_2(): lax.ppermute(tail, axis, [(i, (i + 1) % count) for i in range(ends)])  114 us
    another operation x1, loops' own time, least_squares(): lax.fori_loop(0, columns_total, rotate, (hessenberg, target))  97.8 us
    another operation x46, other arithmetic  30.6 us
    another operation x1, loops' own time, least_squares(): lax.fori_loop(0, columns_total, substitute, jnp.zeros((columns_total,), j...  30.2 us
    ppermute x34, waiting for transfers between devices, padded_2(): lax.ppermute(head, axis, [((i + 1) % count, i) for i in range(ends)])  27.7 us
    dot_general x15, matrix products, arnoldi(): jnp.einsum('kxy,xy->k', basis, applied, precision=lax.Precision.HIGHEST)  26.6 us
  transfers between devices with their start and end apart: 68, of which 64 were waited for; matrix products, arithmetic and copies ran while one was open for 0% of the time, Pallas kernels for 0%

commit v1 on v0

v1 whole, which is shorter than its diff:
```python
import functools

import jax
import jax.numpy as jnp
import numpy as np
from jax import lax
from jax.experimental import pallas as pl
from jax.experimental.pallas import tpu as pltpu
from jax.sharding import PartitionSpec as P

MESH = pl.DeviceIdType.MESH
STEPS = 15
CHUNK = 32
F32 = jnp.float32


def recurrence():
    count = 128
    angle = (np.arange(count) + 0.5) * np.pi / count
    one = (30.0 - 32.0 * np.cos(angle) + 2.0 * np.cos(2.0 * angle)) / 12.0
    values = (0.2 + one[:, None] + one[None, :]).ravel()
    weight = values * values
    scale = 4.0 / (values.max() - values.min())
    values = values * scale
    before, now, norm_before = np.zeros_like(values), np.ones_like(values), 1.0
    centres, links = [], []
    for k in range(STEPS):
        norm = (weight * now * now).sum()
        centre = (weight * values * now * now).sum() / norm
        link = norm / norm_before if k else 0.0
        centres.append(float(centre))
        links.append(float(link))
        before, now, norm_before = now, (values - centre) * now - link * before, norm
    return float(scale), centres, links


SCALE, CENTRES, LINKS = recurrence()

BLOCKS = [(i, j) for i in range(4) for j in range(i, 4)]
SLOT = {}
for number, (bi, bj) in enumerate(BLOCKS):
    for a in range(4):
        for b in range(4):
            SLOT.setdefault((4 * bi + a, 4 * bj + b), number * 16 + a * 4 + b)


def lanes(shape):
    return lax.broadcasted_iota(jnp.int32, shape, 1)


def kernel(gy, *refs):
    ins, outs = refs[:5], refs[5:7]
    (buf, send, halo, speed, coef, field, image, acc, msg, every, spread, done, table,
     in_sem, part_sem, edge_sem, halo_sem, sum_sem, out_sem, far_sem) = refs[7:]
    c = lax.axis_index("gx")
    g = lax.axis_index("gy")
    n = 2 * gy
    me = c * gy + g
    mine = pl.multiple_of(c * 64, 64)
    theirs = pl.multiple_of((1 - c) * 64, 64)
    my_cols = pl.multiple_of(c * 128, 128)

    loads = [pltpu.make_async_copy(ins[q], buf.at[q, pl.ds(mine, 64)], in_sem.at[q]) for q in range(5)]
    for load in loads:
        load.start()

    barrier = pltpu.get_barrier_semaphore()

    def greet(step, carry):
        to = lax.rem(me + step, n)
        pl.semaphore_signal(barrier, inc=1, device_id=(to // gy, lax.rem(to, gy)), device_id_type=MESH)
        return carry

    lax.fori_loop(1, n, greet, 0)

    for k in range(STEPS):
        table[0, k] = CENTRES[k]
        table[1, k] = LINKS[k]
    for load in loads:
        load.wait()

    lane64 = lanes((64, 128))
    lane16 = lanes((16, 128))
    for way in range(2):
        tile, first = (1, 96) if way == 0 else (0, 0)
        packed = None
        for q in range(4):
            at = 32 * (q if way == 0 else (q + 1) % 4)
            piece = buf[q, pl.ds(mine, 64), pl.ds(128 * tile, 128)]
            shift = (at - first) % 128
            piece = pltpu.roll(piece, shift, 1) if shift else piece
            packed = piece if packed is None else jnp.where((lane64 >= at) & (lane64 < at + 32), piece, packed)
        send[way, pl.ds(0, 64)] = packed
        packed = None
        for q in range(4):
            at = 32 * (q if way == 0 else (q + 1) % 4)
            piece = buf[4, pl.ds(pl.multiple_of(mine + 16 * q, 16), 16), pl.ds(128 * tile, 128)]
            shift = (at - first) % 128
            piece = pltpu.roll(piece, shift, 1) if shift else piece
            packed = piece if packed is None else jnp.where((lane16 >= at) & (lane16 < at + 32), piece, packed)
        send[way, pl.ds(64, 16)] = packed

    pl.semaphore_wait(barrier, n - 1)

    edges = []
    for way, (core, chip) in enumerate(((0, lax.rem(g + 1, gy)), (1, lax.rem(g + gy - 1, gy)))):
        edge = pltpu.make_async_remote_copy(
            send.at[way], halo.at[c], edge_sem.at[way], halo_sem.at[c], device_id=(core, chip), device_id_type=MESH
        )
        edge.start()
        edges.append(edge)
    part = pltpu.make_async_remote_copy(
        buf.at[:, pl.ds(mine, 64)], buf.at[:, pl.ds(mine, 64)], part_sem.at[0], part_sem.at[1],
        device_id=(1 - c, g), device_id_type=MESH,
    )
    part.start()
    part.wait()
    for side in range(2):
        pltpu.make_async_copy(halo.at[side], halo.at[side], halo_sem.at[side]).wait()

    def gather(q, rows):
        side = rows // 64
        low = rows % 64
        lane = lanes((CHUNK, 128))
        own = pltpu.roll(buf[q, pl.ds(rows, CHUNK), pl.ds(my_cols, 128)], 32, 1)
        near = pltpu.roll(buf[q, pl.ds(rows, CHUNK), pl.ds(pl.multiple_of(128 - my_cols, 128), 128)], 32, 1)
        if q < 4:
            far = halo[side, pl.ds(low, CHUNK)]
            far = pltpu.roll(far, 128 - 32 * q, 1) if q else far
        else:
            pieces = []
            for k in range(low // 16, low // 16 + CHUNK // 16):
                piece = halo[side, pl.ds(64, 16)]
                pieces.append(pltpu.roll(piece, 128 - 32 * k, 1) if k else piece)
            far = jnp.concatenate(pieces, axis=0)
        edge = jnp.where((lane < 32).astype(jnp.int32) == (1 - c), far, near)
        return jnp.where(lane < 32, edge, own), jnp.where((lane >= 32) & (lane < 64), edge, own)

    def put(ref, at, rows, value):
        ref[at + (pl.ds(8 + rows, CHUNK),)] = value
        if rows == 0:
            ref[at + (pl.ds(136, 8),)] = value[:8]
        if rows == 128 - CHUNK:
            ref[at + (pl.ds(0, 8),)] = value[CHUNK - 8 :]

    ROWS = range(0, 128, CHUNK)
    for rows in ROWS:
        for tile, value in enumerate(gather(1, rows)):
            put(field, (0, tile), rows, value)
        for tile, value in enumerate(gather(3, rows)):
            put(speed, (tile,), rows, value)
    for rows in ROWS:
        here = pl.ds(rows, CHUNK)
        reaction = gather(2, rows)
        along = gather(4, rows)
        for tile in range(2):
            coef[0, tile, here] = SCALE * (reaction[tile] + 5.0)
            vx = speed[tile, pl.ds(8 + rows, CHUNK)]
            for number, (offset, flat, slope) in enumerate(STENCIL):
                other = speed[tile, pl.ds(8 + rows + offset, CHUNK)]
                coef[1 + number, tile, here] = flat + slope * (vx + other)
            vy = along[tile]
            for number, (offset, flat, slope) in enumerate(STENCIL):
                other = pltpu.roll(vy, (-offset) % 128, 1)
                coef[5 + number, tile, here] = flat + slope * (vy + other)

    def operate(slot, tile, rows):
        here = pl.ds(rows, CHUNK)
        centre = field[slot, tile, pl.ds(8 + rows, CHUNK)]
        total = coef[0, tile, here] * centre
        for number, (offset, _, _) in enumerate(STENCIL):
            total = total + coef[1 + number, tile, here] * field[slot, tile, pl.ds(8 + rows + offset, CHUNK)]
        for number, (offset, _, _) in enumerate(STENCIL):
            total = total + coef[5 + number, tile, here] * pltpu.roll(centre, (-offset) % 128, 1)
        return centre, total

    def core(lane, first, second):
        return jnp.where((lane >= 32) & (lane < 96), first, second)

    lane = lanes((CHUNK, 128))
    for rows in ROWS:
        right = gather(0, rows)
        start = []
        for tile in range(2):
            _, total = operate(0, tile, rows)
            value = right[tile] - (1.0 / SCALE) * total
            put(field, (1, tile), rows, value)
            start.append(value)
        image[STEPS, pl.ds(rows, CHUNK)] = core(lane, *start)

    def step(k, carry):
        centre_k = table[0, k]
        link_k = table[1, k]
        for rows in ROWS:
            both = []
            for tile in range(2):
                now, total = operate(k + 1, tile, rows)
                before = field[k, tile, pl.ds(8 + rows, CHUNK)]
                put(field, (k + 2, tile), rows, total - centre_k * now - link_k * before)
                both.append(total)
            image[k, pl.ds(rows, CHUNK)] = core(lane, *both)
        return carry

    lax.fori_loop(0, STEPS, step, 0)

    for number, (bi, bj) in enumerate(BLOCKS):

        def products(row, sums, bi=bi, bj=bj):
            at = pl.ds(pl.multiple_of(row * 8, 8), 8)
            left = [image[4 * bi + a, at] for a in range(4)]
            right = left if bi == bj else [image[4 * bj + b, at] for b in range(4)]
            return tuple(sums[4 * a + b] + left[a] * right[b] for a in range(4) for b in range(4))

        sums = lax.fori_loop(0, 16, products, (jnp.zeros((8, 128), F32),) * 16)
        for a in range(16):
            acc[number * 16 + a] = sums[a]

    totals = jnp.sum(jnp.sum(acc[...], axis=1), axis=1, keepdims=True)
    wide = jnp.broadcast_to(totals[:128], (128, 128))
    pick = lax.broadcasted_iota(jnp.int32, (128, 128), 0) == lanes((128, 128))
    msg[pl.ds(0, 1)] = jnp.sum(jnp.where(pick, wide, 0.0), axis=0, keepdims=True)
    wide = jnp.broadcast_to(totals[128:], (32, 128))
    msg[pl.ds(1, 1)] = jnp.sum(jnp.where(pick[:32], wide, 0.0), axis=0, keepdims=True)

    def tell(step, carry):
        to = lax.rem(me + step, n)
        pltpu.make_async_remote_copy(
            msg, every.at[me], sum_sem.at[0], sum_sem.at[1],
            device_id=(to // gy, lax.rem(to, gy)), device_id_type=MESH,
        ).start()
        return carry

    lax.fori_loop(1, n, tell, 0)
    every[me] = msg[...]
    others = every.at[pl.ds(0, n - 1)]
    pltpu.make_async_copy(others, others, sum_sem.at[1]).wait()
    total = jnp.sum(every[...], axis=0)

    wide = jnp.where(pick, jnp.broadcast_to(total[0:1], (128, 128)), 0.0)
    spread[pl.ds(0, 128)] = jnp.broadcast_to(jnp.sum(wide, axis=1, keepdims=True), (128, 128))
    wide = jnp.where(pick[:32], jnp.broadcast_to(total[1:2], (32, 128)), 0.0)
    spread[pl.ds(128, 32)] = jnp.broadcast_to(jnp.sum(wide, axis=1, keepdims=True), (32, 128))

    def entry(i, j):
        at = SLOT[(min(i, j), max(i, j))]
        return jnp.broadcast_to(spread[at : at + 1], (8, 128))

    gram = [[entry(i, j) for j in range(i + 1)] for i in range(STEPS)]
    goal = [entry(i, STEPS) for i in range(STEPS)]
    inverse = []
    for k in range(STEPS):
        inverse.append(1.0 / gram[k][k])
        for i in range(k + 1, STEPS):
            ratio = gram[i][k] * inverse[k]
            for j in range(k + 1, i + 1):
                gram[i][j] = gram[i][j] - ratio * gram[j][k]
            goal[i] = goal[i] - ratio * goal[k]
    weights = [None] * STEPS
    for k in reversed(range(STEPS)):
        value = goal[k]
        for i in range(k + 1, STEPS):
            value = value - gram[i][k] * weights[i]
        weights[k] = value * inverse[k]

    lane8 = lanes((8, 128))

    def finish(row, carry):
        at = pl.ds(pl.multiple_of(row * 8, 8), 8)
        inner = pl.ds(pl.multiple_of(row * 8 + 8, 8), 8)
        leftover = image[STEPS, at]
        change = jnp.zeros((8, 128), F32)
        for k in range(STEPS):
            leftover = leftover - weights[k] * image[k, at]
            change = change + weights[k] * core(lane8, field[k + 1, 0, inner], field[k + 1, 1, inner])
        start = core(lane8, field[0, 0, inner], field[0, 1, inner])
        done[0, at] = pltpu.roll(start + SCALE * change, 96, 1)
        done[1, at] = pltpu.roll(leftover, 96, 1)
        return carry

    lax.fori_loop(0, 16, finish, 0)

    ends = []
    for o in range(2):
        away = pltpu.make_async_remote_copy(
            done.at[o, pl.ds(theirs, 64)], outs[o].at[:, pl.ds(my_cols, 128)], far_sem.at[0, o], far_sem.at[1, o],
            device_id=(1 - c, g), device_id_type=MESH,
        )
        away.start()
        home = pltpu.make_async_copy(done.at[o, pl.ds(mine, 64)], outs[o].at[:, pl.ds(my_cols, 128)], out_sem.at[o])
        home.start()
        ends += [away, home]
    for end in ends:
        end.wait()
    for edge in edges:
        edge.wait_send()
    pltpu.make_async_copy(others, others, sum_sem.at[0]).wait()


STENCIL = [
    (-2, SCALE / 12.0, SCALE / 24.0),
    (-1, -SCALE * 16.0 / 12.0, -SCALE * 8.0 / 24.0),
    (1, -SCALE * 16.0 / 12.0, SCALE * 8.0 / 24.0),
    (2, SCALE / 12.0, -SCALE / 24.0),
]


def solution(mesh):
    gy = mesh.shape["gy"]
    n = 2 * gy
    anywhere = pl.BlockSpec(memory_space=pl.ANY)

    def per_device(*blocks):
        return pl.pallas_call(
            functools.partial(kernel, gy),
            out_shape=[jax.ShapeDtypeStruct((64, 256), F32)] * 2,
            in_specs=[anywhere] * 5,
            out_specs=[anywhere] * 2,
            scratch_shapes=[
                pltpu.VMEM((5, 128, 256), F32),
                pltpu.VMEM((2, 80, 128), F32),
                pltpu.VMEM((2, 80, 128), F32),
                pltpu.VMEM((2, 144, 128), F32),
                pltpu.VMEM((9, 2, 128, 128), F32),
                pltpu.VMEM((STEPS + 2, 2, 144, 128), F32),
                pltpu.VMEM((STEPS + 1, 128, 128), F32),
                pltpu.VMEM((160, 8, 128), F32),
                pltpu.VMEM((2, 128), F32),
                pltpu.VMEM((n, 2, 128), F32),
                pltpu.VMEM((160, 128), F32),
                pltpu.VMEM((2, 128, 128), F32),
                pltpu.SMEM((2, 16), F32),
                pltpu.SemaphoreType.DMA((5,)),
                pltpu.SemaphoreType.DMA((2,)),
                pltpu.SemaphoreType.DMA((2,)),
                pltpu.SemaphoreType.DMA((2,)),
                pltpu.SemaphoreType.DMA((2,)),
                pltpu.SemaphoreType.DMA((2,)),
                pltpu.SemaphoreType.DMA((2, 2)),
            ],
            compiler_params=pltpu.CompilerParams(collective_id=0, has_side_effects=True),
        )(*blocks)

    placed = P("gx", "gy")
    return jax.shard_map(
        per_device, mesh=mesh, in_specs=(placed,) * 5, out_specs=(placed, placed), check_vma=False
    )
```

time: 1040 us -> 35 us (0.03)
  blocking collectives: 398 us -> 0 us
  starting transfers between devices: 167 us -> 0 us
  loops' own time: 149 us -> 0 us
  waiting for transfers between devices: 141 us -> 0 us
  other arithmetic: 84.3 us -> 0 us
  matrix products: 46.7 us -> 0 us
  local copies, waits for them, and re-layouts: 42.3 us -> 2.14 us
  Pallas kernels: 0 us -> 32 us
    psum x64 -> x0, blocking collectives: 398 us -> none  [one_axis_at_a_time(): x = lax.psum(x, axis)]
    ppermute x68 -> x0, starting transfers between devices: 167 us -> none  [the longest x34 163 us: padded_2(): lax.ppermute(head, axis, [((i + 1) % count, i) for i in range(ends)])]
    another operation x3 -> x0, loops' own time: 149 us -> none  [the longest x1 97.8 us: least_squares(): lax.fori_loop(0, columns_total, rotate, (hessenberg, target))]
    ppermute x68 -> x0, waiting for transfers between devices: 141 us -> none  [the longest x34 114 us: padded_2(): lax.ppermute(tail, axis, [(i, (i + 1) % count) for i in range(ends)])]
    dot_general x33 -> x0, matrix products: 46.7 us -> none  [the longest x15 26.6 us: arnoldi(): jnp.einsum('kxy,xy->k', basis, applied, precision=lax.Precision.HIGHEST)]
    dynamic_slice x60 -> x0, local copies, waits for them, and re-layouts: 36.8 us -> none  [the longest x15 9.87 us: rotate(): diagonal_entry = top_row[column]]
    reduce_sum x46 -> x0, other arithmetic: 32.2 us -> none  [the longest x15 12.9 us: arnoldi(): jnp.sum(applied * applied)]
    pallas_call x0 -> x1, Pallas kernels: none -> 32 us  [per_device(): pl.pallas_call(functools.partial(kernel, gy), out_shape=[jax.ShapeDtypeSt...]
  transfers between devices with their start and end apart: 68 -> 0, of which waited for: 64 -> 0; matrix products, arithmetic and copies ran while one was open for 0% -> 0% of each run, Pallas kernels for 0% -> 0%
where the time goes in v1:
time: 35 us; the launch traced here: 34.8 us
  Pallas kernels  32 us (91%)
  local copies, waits for them, and re-layouts  2.14 us (6%)
  between operations  0.65 us (2%)
    pallas_call x1, Pallas kernels, per_device(): pl.pallas_call(functools.partial(kernel, gy), out_shape=[jax.ShapeDtypeSt...  32 us
    unnamed x4, local copies, waits for them, and re-layouts  2.14 us

profile of v1, /device:TPU:1, one launch (start us, length us, event | category | flops | bytes accessed | tf_op | source)
XLA Modules:
  0.0 34.8 jit_solution(1593252431962385888)
XLA Ops:
  0.6 32.0 %shard_map.68 = (f32[64,256]{1,0:T(8,128)}, f32[64,256]{1,0:T(8,128)}) custom-call(f32[64,256]{1,0:T(8,128)} %refs_0_.1, f32[64,256]{1,0:T(8,128)} %refs_1_.1, f32[64,256]{1,0:T(8,128)} %refs_2_.1, f32[64,256]{1,0:T(8,128)} %refs_3_.1, f32[64,256]{1,0:T(8,128)} %refs_4_.1), custom_call_target="tpu_custom_call" | custom-call | tf_op jit(solution)/shard_map/pallas_call | solution.py:313
  32.7 0.0 copy-start
  32.7 1.5 %copy.9 = f32[64,256]{1,0:T(8,128)} copy(f32[64,256]{1,0:T(8,128)} %get-tuple-element.4) | data formatting | bytes 131072
  34.2 0.0 copy-done
  34.2 0.6 %copy.10 = f32[64,256]{1,0:T(8,128)} copy(f32[64,256]{1,0:T(8,128)S(1)} %copy-done) | data formatting | bytes 131072
Async XLA Ops:
  32.7 1.5 %copy-start = (f32[64,256]{1,0:T(8,128)S(1)}, f32[64,256]{1,0:T(8,128)}, u32[]{:S(2)}) copy-start(f32[64,256]{1,0:T(8,128)} %get-tuple-element.5) | copy-start | bytes 196612

commit v2 on v1

--- a/solution.py
+++ b/solution.py
@@ -51,7 +51,7 @@
 def kernel(gy, *refs):
     ins, outs = refs[:5], refs[5:7]
     (buf, send, halo, speed, coef, field, image, acc, msg, every, spread, done, table,
-     in_sem, part_sem, edge_sem, halo_sem, sum_sem, out_sem, far_sem) = refs[7:]
+     in_sem, part_sem, edge_sem, halo_sem, sum_sem, out_sem, far_sem, meet) = refs[7:]
     c = lax.axis_index("gx")
     g = lax.axis_index("gy")
     n = 2 * gy
@@ -64,14 +64,26 @@
     for load in loads:
         load.start()
 
+    sizes = (4, 4, 4) if gy == 64 else (1, 2, gy // 2)
+    strides = (sizes[1] * sizes[2], sizes[2], 1)
+    around = [
+        [lax.rem(lax.rem(g // stride, size) + k, size) * stride for k in range(size)]
+        for stride, size in zip(strides, sizes)
+    ]
+    ahead, behind = lax.rem(g + 1, gy), lax.rem(g + gy - 1, gy)
+
+    def line(d):
+        rest = g - around[d][0]
+        return [(c, rest + around[d][k]) for k in sorted(range(1, sizes[d]), key=lambda k: k != sizes[d] // 2)]
+
+    def signal(sem, to):
+        pl.semaphore_signal(sem, inc=1, device_id=to, device_id_type=MESH)
+
     barrier = pltpu.get_barrier_semaphore()
-
-    def greet(step, carry):
-        to = lax.rem(me + step, n)
-        pl.semaphore_signal(barrier, inc=1, device_id=(to // gy, lax.rem(to, gy)), device_id_type=MESH)
-        return carry
-
-    lax.fori_loop(1, n, greet, 0)
+    sender = jnp.where(c == 0, behind, ahead)
+    greeted = [(0, sender), (1, sender)] + line(0) + line(1) + line(2) + [(1 - c, g)]
+    for to in greeted:
+        signal(barrier, to)
 
     for k in range(STEPS):
         table[0, k] = CENTRES[k]
@@ -100,10 +112,10 @@
             packed = piece if packed is None else jnp.where((lane16 >= at) & (lane16 < at + 32), piece, packed)
         send[way, pl.ds(64, 16)] = packed
 
-    pl.semaphore_wait(barrier, n - 1)
+    pl.semaphore_wait(barrier, len(greeted))
 
     edges = []
-    for way, (core, chip) in enumerate(((0, lax.rem(g + 1, gy)), (1, lax.rem(g + gy - 1, gy)))):
+    for way, (core, chip) in enumerate(((0, ahead), (1, behind))):
         edge = pltpu.make_async_remote_copy(
             send.at[way], halo.at[c], edge_sem.at[way], halo_sem.at[c], device_id=(core, chip), device_id_type=MESH
         )
@@ -114,10 +126,15 @@
         device_id=(1 - c, g), device_id_type=MESH,
     )
     part.start()
+    for to in line(2):
+        signal(meet.at[0], to)
     part.wait()
     for side in range(2):
         pltpu.make_async_copy(halo.at[side], halo.at[side], halo_sem.at[side]).wait()
 
+    pl.semaphore_wait(meet.at[0], sizes[2] - 1)
+    for to in line(1):
+        signal(meet.at[1], to)
     def gather(q, rows):
         side = rows // 64
         low = rows % 64
@@ -188,6 +205,9 @@
             start.append(value)
         image[STEPS, pl.ds(rows, CHUNK)] = core(lane, *start)
 
+    pl.semaphore_wait(meet.at[1], sizes[1] - 1)
+    for to in line(0):
+        signal(meet.at[2], to)
     def step(k, carry):
         centre_k = table[0, k]
         link_k = table[1, k]
@@ -222,15 +242,17 @@
     wide = jnp.broadcast_to(totals[128:], (32, 128))
     msg[pl.ds(1, 1)] = jnp.sum(jnp.where(pick[:32], wide, 0.0), axis=0, keepdims=True)
 
-    def tell(step, carry):
-        to = lax.rem(me + step, n)
+    pl.semaphore_wait(meet.at[2], sizes[0] - 1)
+
+    def hops(way):
+        return sum(min(k, size - k) for k, size in zip(way[:3], sizes)) + 0.5 * way[3]
+
+    ways = [(z, y, x, w) for z in range(sizes[0]) for y in range(sizes[1]) for x in range(sizes[2]) for w in range(2)]
+    for z, y, x, w in sorted(ways[1:], key=hops, reverse=True):
         pltpu.make_async_remote_copy(
             msg, every.at[me], sum_sem.at[0], sum_sem.at[1],
-            device_id=(to // gy, lax.rem(to, gy)), device_id_type=MESH,
+            device_id=(1 - c if w else c, around[0][z] + around[1][y] + around[2][x]), device_id_type=MESH,
         ).start()
-        return carry
-
-    lax.fori_loop(1, n, tell, 0)
     every[me] = msg[...]
     others = every.at[pl.ds(0, n - 1)]
     pltpu.make_async_copy(others, others, sum_sem.at[1]).wait()
@@ -336,6 +358,7 @@
                 pltpu.SemaphoreType.DMA((2,)),
                 pltpu.SemaphoreType.DMA((2,)),
                 pltpu.SemaphoreType.DMA((2, 2)),
+                pltpu.SemaphoreType.REGULAR((3,)),
             ],
             compiler_params=pltpu.CompilerParams(collective_id=0, has_side_effects=True),
         )(*blocks)

time: 35 us -> 32.1 us (0.917)
  Pallas kernels: 32 us -> 29.1 us
    pallas_call x1, Pallas kernels: 32 us -> 29.1 us  [per_device(): pl.pallas_call(functools.partial(kernel, gy), out_shape=[jax.ShapeDtypeSt...]
where the time goes in v2:
time: 32.1 us; the launch traced here: 31.8 us
  Pallas kernels  29.1 us (91%)
  local copies, waits for them, and re-layouts  2.14 us (7%)
  between operations  0.65 us (2%)
    pallas_call x1, Pallas kernels, per_device(): pl.pallas_call(functools.partial(kernel, gy), out_shape=[jax.ShapeDtypeSt...  29.1 us
    unnamed x4, local copies, waits for them, and re-layouts  2.14 us

profile of v2, /device:TPU:1, one launch (start us, length us, event | category | flops | bytes accessed | tf_op | source)
XLA Modules:
  0.0 31.8 jit_solution(15862748398938962628)
XLA Ops:
  0.6 29.1 %shard_map.68 = (f32[64,256]{1,0:T(8,128)}, f32[64,256]{1,0:T(8,128)}) custom-call(f32[64,256]{1,0:T(8,128)} %refs_0_.1, f32[64,256]{1,0:T(8,128)} %refs_1_.1, f32[64,256]{1,0:T(8,128)} %refs_2_.1, f32[64,256]{1,0:T(8,128)} %refs_3_.1, f32[64,256]{1,0:T(8,128)} %refs_4_.1), custom_call_target="tpu_custom_call" | custom-call | tf_op jit(solution)/shard_map/pallas_call | solution.py:335
  29.7 0.0 copy-start
  29.7 1.5 %copy.9 = f32[64,256]{1,0:T(8,128)} copy(f32[64,256]{1,0:T(8,128)} %get-tuple-element.4) | data formatting | bytes 131072
  31.2 0.0 copy-done
  31.2 0.6 %copy.10 = f32[64,256]{1,0:T(8,128)} copy(f32[64,256]{1,0:T(8,128)S(1)} %copy-done) | data formatting | bytes 131072
Async XLA Ops:
  29.7 1.5 %copy-start = (f32[64,256]{1,0:T(8,128)S(1)}, f32[64,256]{1,0:T(8,128)}, u32[]{:S(2)}) copy-start(f32[64,256]{1,0:T(8,128)} %get-tuple-element.5) | copy-start | bytes 196612

commit v3 on v2

--- a/solution.py
+++ b/solution.py
@@ -50,8 +50,8 @@
 
 def kernel(gy, *refs):
     ins, outs = refs[:5], refs[5:7]
-    (buf, send, halo, speed, coef, field, image, acc, msg, every, spread, done, table,
-     in_sem, part_sem, edge_sem, halo_sem, sum_sem, out_sem, far_sem, meet) = refs[7:]
+    (buf, send, halo, plain, edge, speed, coef, field, image, acc, msg, every, spread, done, table,
+     in_sem, part_sem, edge_sem, halo_sem, sum_sem, far_sem, meet) = refs[7:]
     c = lax.axis_index("gx")
     g = lax.axis_index("gy")
     n = 2 * gy
@@ -81,7 +81,8 @@
 
     barrier = pltpu.get_barrier_semaphore()
     sender = jnp.where(c == 0, behind, ahead)
-    greeted = [(0, sender), (1, sender)] + line(0) + line(1) + line(2) + [(1 - c, g)]
+    across = [(1 - c, chip) for _, chip in line(0)]
+    greeted = [(0, sender), (1, sender)] + line(0) + across + line(1) + line(2) + [(1 - c, g)]
     for to in greeted:
         signal(barrier, to)
 
@@ -116,11 +117,11 @@
 
     edges = []
     for way, (core, chip) in enumerate(((0, ahead), (1, behind))):
-        edge = pltpu.make_async_remote_copy(
+        copy = pltpu.make_async_remote_copy(
             send.at[way], halo.at[c], edge_sem.at[way], halo_sem.at[c], device_id=(core, chip), device_id_type=MESH
         )
-        edge.start()
-        edges.append(edge)
+        copy.start()
+        edges.append(copy)
     part = pltpu.make_async_remote_copy(
         buf.at[:, pl.ds(mine, 64)], buf.at[:, pl.ds(mine, 64)], part_sem.at[0], part_sem.at[1],
         device_id=(1 - c, g), device_id_type=MESH,
@@ -128,30 +129,15 @@
     part.start()
     for to in line(2):
         signal(meet.at[0], to)
+    lane = lanes((CHUNK, 128))
+    ROWS = range(0, 128, CHUNK)
+    near = pl.multiple_of(128 - my_cols, 128)
     part.wait()
-    for side in range(2):
-        pltpu.make_async_copy(halo.at[side], halo.at[side], halo_sem.at[side]).wait()
-
-    pl.semaphore_wait(meet.at[0], sizes[2] - 1)
-    for to in line(1):
-        signal(meet.at[1], to)
-    def gather(q, rows):
-        side = rows // 64
-        low = rows % 64
-        lane = lanes((CHUNK, 128))
-        own = pltpu.roll(buf[q, pl.ds(rows, CHUNK), pl.ds(my_cols, 128)], 32, 1)
-        near = pltpu.roll(buf[q, pl.ds(rows, CHUNK), pl.ds(pl.multiple_of(128 - my_cols, 128), 128)], 32, 1)
-        if q < 4:
-            far = halo[side, pl.ds(low, CHUNK)]
-            far = pltpu.roll(far, 128 - 32 * q, 1) if q else far
-        else:
-            pieces = []
-            for k in range(low // 16, low // 16 + CHUNK // 16):
-                piece = halo[side, pl.ds(64, 16)]
-                pieces.append(pltpu.roll(piece, 128 - 32 * k, 1) if k else piece)
-            far = jnp.concatenate(pieces, axis=0)
-        edge = jnp.where((lane < 32).astype(jnp.int32) == (1 - c), far, near)
-        return jnp.where(lane < 32, edge, own), jnp.where((lane >= 32) & (lane < 64), edge, own)
+    for q in range(5):
+        for rows in ROWS:
+            here = pl.ds(rows, CHUNK)
+            plain[q, here] = pltpu.roll(buf[q, here, pl.ds(my_cols, 128)], 32, 1)
+            edge[q, here] = pltpu.roll(buf[q, here, pl.ds(near, 128)], 32, 1)
 
     def put(ref, at, rows, value):
         ref[at + (pl.ds(8 + rows, CHUNK),)] = value
@@ -160,78 +146,89 @@
         if rows == 128 - CHUNK:
             ref[at + (pl.ds(0, 8),)] = value[CHUNK - 8 :]
 
-    ROWS = range(0, 128, CHUNK)
-    for rows in ROWS:
-        for tile, value in enumerate(gather(1, rows)):
-            put(field, (0, tile), rows, value)
-        for tile, value in enumerate(gather(3, rows)):
-            put(speed, (tile,), rows, value)
-    for rows in ROWS:
-        here = pl.ds(rows, CHUNK)
-        reaction = gather(2, rows)
-        along = gather(4, rows)
-        for tile in range(2):
-            coef[0, tile, here] = SCALE * (reaction[tile] + 5.0)
-            vx = speed[tile, pl.ds(8 + rows, CHUNK)]
-            for number, (offset, flat, slope) in enumerate(STENCIL):
-                other = speed[tile, pl.ds(8 + rows + offset, CHUNK)]
-                coef[1 + number, tile, here] = flat + slope * (vx + other)
-            vy = along[tile]
-            for number, (offset, flat, slope) in enumerate(STENCIL):
-                other = pltpu.roll(vy, (-offset) % 128, 1)
-                coef[5 + number, tile, here] = flat + slope * (vy + other)
-
     def operate(slot, tile, rows):
         here = pl.ds(rows, CHUNK)
         centre = field[slot, tile, pl.ds(8 + rows, CHUNK)]
-        total = coef[0, tile, here] * centre
+        total = coef[0, here] * centre
         for number, (offset, _, _) in enumerate(STENCIL):
-            total = total + coef[1 + number, tile, here] * field[slot, tile, pl.ds(8 + rows + offset, CHUNK)]
+            total = total + coef[1 + number, here] * field[slot, tile, pl.ds(8 + rows + offset, CHUNK)]
         for number, (offset, _, _) in enumerate(STENCIL):
-            total = total + coef[5 + number, tile, here] * pltpu.roll(centre, (-offset) % 128, 1)
+            total = total + coef[5 + number, here] * pltpu.roll(centre, (-offset) % 128, 1)
         return centre, total
 
-    def core(lane, first, second):
-        return jnp.where((lane >= 32) & (lane < 96), first, second)
-
-    lane = lanes((CHUNK, 128))
-    for rows in ROWS:
-        right = gather(0, rows)
-        start = []
-        for tile in range(2):
+    def half(phase, carry):
+        tile = lax.rem(1 - c + phase, 2)
+
+        @pl.when(phase == 1)
+        def _():
+            for side in range(2):
+                pltpu.make_async_copy(halo.at[side], halo.at[side], halo_sem.at[side]).wait()
+            for side in range(2):
+                for q in range(4):
+                    far = halo[side, pl.ds(0, 64)]
+                    edge[q, pl.ds(64 * side, 64)] = pltpu.roll(far, 128 - 32 * q, 1) if q else far
+                for q in range(4):
+                    far = halo[side, pl.ds(64, 16)]
+                    edge[4, pl.ds(64 * side + 16 * q, 16)] = pltpu.roll(far, 128 - 32 * q, 1) if q else far
+            pl.semaphore_wait(meet.at[0], sizes[2] - 1)
+            for to in line(1):
+                signal(meet.at[1], to)
+
+        halo_lanes = (lane >= 32 * tile) & (lane < 32 * tile + 32)
+        core_lanes = ((lane >= 32) & (lane < 96)).astype(jnp.int32) == 1 - tile
+
+        def gather(q, rows):
+            here = pl.ds(rows, CHUNK)
+            return jnp.where(halo_lanes, edge[q, here], plain[q, here])
+
+        for rows in ROWS:
+            put(field, (0, tile), rows, gather(1, rows))
+            put(speed, (), rows, gather(3, rows))
+        for rows in ROWS:
+            here = pl.ds(rows, CHUNK)
+            coef[0, here] = SCALE * (gather(2, rows) + 5.0)
+            vx = speed[pl.ds(8 + rows, CHUNK)]
+            for number, (offset, flat, slope) in enumerate(STENCIL):
+                other = speed[pl.ds(8 + rows + offset, CHUNK)]
+                coef[1 + number, here] = flat + slope * (vx + other)
+            vy = gather(4, rows)
+            for number, (offset, flat, slope) in enumerate(STENCIL):
+                other = pltpu.roll(vy, (-offset) % 128, 1)
+                coef[5 + number, here] = flat + slope * (vy + other)
+        for rows in ROWS:
             _, total = operate(0, tile, rows)
-            value = right[tile] - (1.0 / SCALE) * total
+            value = gather(0, rows) - (1.0 / SCALE) * total
             put(field, (1, tile), rows, value)
-            start.append(value)
-        image[STEPS, pl.ds(rows, CHUNK)] = core(lane, *start)
-
-    pl.semaphore_wait(meet.at[1], sizes[1] - 1)
-    for to in line(0):
-        signal(meet.at[2], to)
-    def step(k, carry):
-        centre_k = table[0, k]
-        link_k = table[1, k]
-        for rows in ROWS:
-            both = []
-            for tile in range(2):
+            pltpu.store(image.at[STEPS, pl.ds(rows, CHUNK)], value, mask=core_lanes)
+
+        def step(k, carry):
+            centre_k = table[0, k]
+            link_k = table[1, k]
+            for rows in ROWS:
                 now, total = operate(k + 1, tile, rows)
                 before = field[k, tile, pl.ds(8 + rows, CHUNK)]
                 put(field, (k + 2, tile), rows, total - centre_k * now - link_k * before)
-                both.append(total)
-            image[k, pl.ds(rows, CHUNK)] = core(lane, *both)
-        return carry
-
-    lax.fori_loop(0, STEPS, step, 0)
+                pltpu.store(image.at[k, pl.ds(rows, CHUNK)], total, mask=core_lanes)
+            return carry
+
+        return lax.fori_loop(0, STEPS, step, carry)
+
+    lax.fori_loop(0, 2, half, 0)
+
+    def core(lane, first, second):
+        return jnp.where((lane >= 32) & (lane < 96), first, second)
 
     for number, (bi, bj) in enumerate(BLOCKS):
 
         def products(row, sums, bi=bi, bj=bj):
-            at = pl.ds(pl.multiple_of(row * 8, 8), 8)
-            left = [image[4 * bi + a, at] for a in range(4)]
-            right = left if bi == bj else [image[4 * bj + b, at] for b in range(4)]
-            return tuple(sums[4 * a + b] + left[a] * right[b] for a in range(4) for b in range(4))
-
-        sums = lax.fori_loop(0, 16, products, (jnp.zeros((8, 128), F32),) * 16)
+            for part in range(4):
+                at = pl.ds(pl.multiple_of(row * 32 + 8 * part, 8), 8)
+                left = [image[4 * bi + a, at] for a in range(4)]
+                right = left if bi == bj else [image[4 * bj + b, at] for b in range(4)]
+                sums = tuple(sums[4 * a + b] + left[a] * right[b] for a in range(4) for b in range(4))
+            return sums
+
+        sums = lax.fori_loop(0, 4, products, (jnp.zeros((8, 128), F32),) * 16)
         for a in range(16):
             acc[number * 16 + a] = sums[a]
 
@@ -242,7 +239,7 @@
     wide = jnp.broadcast_to(totals[128:], (32, 128))
     msg[pl.ds(1, 1)] = jnp.sum(jnp.where(pick[:32], wide, 0.0), axis=0, keepdims=True)
 
-    pl.semaphore_wait(meet.at[2], sizes[0] - 1)
+    pl.semaphore_wait(meet.at[1], sizes[1] - 1)
 
     def hops(way):
         return sum(min(k, size - k) for k, size in zip(way[:3], sizes)) + 0.5 * way[3]
@@ -256,7 +253,12 @@
     every[me] = msg[...]
     others = every.at[pl.ds(0, n - 1)]
     pltpu.make_async_copy(others, others, sum_sem.at[1]).wait()
-    total = jnp.sum(every[...], axis=0)
+    width = n // 2
+    total = every[pl.ds(0, width)] + every[pl.ds(width, width)]
+    while width > 1:
+        width //= 2
+        total = total[:width] + total[width:]
+    total = total[0]
 
     wide = jnp.where(pick, jnp.broadcast_to(total[0:1], (128, 128)), 0.0)
     spread[pl.ds(0, 128)] = jnp.broadcast_to(jnp.sum(wide, axis=1, keepdims=True), (128, 128))
@@ -285,36 +287,42 @@
         weights[k] = value * inverse[k]
 
     lane8 = lanes((8, 128))
-
-    def finish(row, carry):
-        at = pl.ds(pl.multiple_of(row * 8, 8), 8)
-        inner = pl.ds(pl.multiple_of(row * 8 + 8, 8), 8)
-        leftover = image[STEPS, at]
-        change = jnp.zeros((8, 128), F32)
-        for k in range(STEPS):
-            leftover = leftover - weights[k] * image[k, at]
-            change = change + weights[k] * core(lane8, field[k + 1, 0, inner], field[k + 1, 1, inner])
-        start = core(lane8, field[0, 0, inner], field[0, 1, inner])
-        done[0, at] = pltpu.roll(start + SCALE * change, 96, 1)
-        done[1, at] = pltpu.roll(leftover, 96, 1)
-        return carry
-
-    lax.fori_loop(0, 16, finish, 0)
-
-    ends = []
+    inside = (lane8 >= 32) & (lane8 < 96)
+
+    def finish(first):
+        def some(row, carry):
+            for part in range(4):
+                at = pl.ds(pl.multiple_of(first + row * 32 + 8 * part, 8), 8)
+                inner = pl.ds(pl.multiple_of(first + row * 32 + 8 * part + 8, 8), 8)
+                leftover = image[STEPS, at]
+                change = None
+                for k in range(STEPS):
+                    leftover = leftover - weights[k] * image[k, at]
+                    term = weights[k] * jnp.where(inside, field[k + 1, 0, inner], field[k + 1, 1, inner])
+                    change = term if change is None else change + term
+                start = jnp.where(inside, field[0, 0, inner], field[0, 1, inner])
+                done[0, at] = pltpu.roll(start + SCALE * change, 96, 1)
+                done[1, at] = pltpu.roll(leftover, 96, 1)
+            return carry
+
+        lax.fori_loop(0, 2, some, 0)
+
+    finish(theirs)
+    aways = []
     for o in range(2):
         away = pltpu.make_async_remote_copy(
             done.at[o, pl.ds(theirs, 64)], outs[o].at[:, pl.ds(my_cols, 128)], far_sem.at[0, o], far_sem.at[1, o],
             device_id=(1 - c, g), device_id_type=MESH,
         )
         away.start()
-        home = pltpu.make_async_copy(done.at[o, pl.ds(mine, 64)], outs[o].at[:, pl.ds(my_cols, 128)], out_sem.at[o])
-        home.start()
-        ends += [away, home]
-    for end in ends:
-        end.wait()
-    for edge in edges:
-        edge.wait_send()
+        aways.append(away)
+    finish(mine)
+    for o in range(2):
+        outs[o][:, pl.ds(my_cols, 128)] = done[o, pl.ds(mine, 64)]
+    for away in aways:
+        away.wait()
+    for edge_copy in edges:
+        edge_copy.wait_send()
     pltpu.make_async_copy(others, others, sum_sem.at[0]).wait()
 
 
@@ -326,23 +334,34 @@
 ]
 
 
+def write(*refs):
+    moves = [pltpu.make_async_copy(refs[o], refs[2 + o], refs[4].at[o]) for o in range(2)]
+    for move in moves:
+        move.start()
+    for move in moves:
+        move.wait()
+
+
 def solution(mesh):
     gy = mesh.shape["gy"]
     n = 2 * gy
     anywhere = pl.BlockSpec(memory_space=pl.ANY)
 
     def per_device(*blocks):
-        return pl.pallas_call(
+        blocks = [pltpu.with_memory_space_constraint(block, pltpu.HBM) for block in blocks]
+        both = pl.pallas_call(
             functools.partial(kernel, gy),
             out_shape=[jax.ShapeDtypeStruct((64, 256), F32)] * 2,
             in_specs=[anywhere] * 5,
-            out_specs=[anywhere] * 2,
+            out_specs=[pl.BlockSpec(memory_space=pltpu.VMEM)] * 2,
             scratch_shapes=[
                 pltpu.VMEM((5, 128, 256), F32),
                 pltpu.VMEM((2, 80, 128), F32),
                 pltpu.VMEM((2, 80, 128), F32),
-                pltpu.VMEM((2, 144, 128), F32),
-                pltpu.VMEM((9, 2, 128, 128), F32),
+                pltpu.VMEM((5, 128, 128), F32),
+                pltpu.VMEM((5, 128, 128), F32),
+                pltpu.VMEM((144, 128), F32),
+                pltpu.VMEM((9, 128, 128), F32),
                 pltpu.VMEM((STEPS + 2, 2, 144, 128), F32),
                 pltpu.VMEM((STEPS + 1, 128, 128), F32),
                 pltpu.VMEM((160, 8, 128), F32),
@@ -356,12 +375,18 @@
                 pltpu.SemaphoreType.DMA((2,)),
                 pltpu.SemaphoreType.DMA((2,)),
                 pltpu.SemaphoreType.DMA((2,)),
-                pltpu.SemaphoreType.DMA((2,)),
                 pltpu.SemaphoreType.DMA((2, 2)),
-                pltpu.SemaphoreType.REGULAR((3,)),
+                pltpu.SemaphoreType.REGULAR((2,)),
             ],
-            compiler_params=pltpu.CompilerParams(collective_id=0, has_side_effects=True),
+            compiler_params=pltpu.CompilerParams(collective_id=0, has_side_effects=True, vmem_limit_bytes=12 << 20),
         )(*blocks)
+        return pl.pallas_call(
+            write,
+            out_shape=[jax.ShapeDtypeStruct((64, 256), F32)] * 2,
+            in_specs=[anywhere] * 2,
+            out_specs=[anywhere] * 2,
+            scratch_shapes=[pltpu.SemaphoreType.DMA((2,))],
+        )(*[pltpu.with_memory_space_constraint(one, pltpu.VMEM) for one in both])
 
     placed = P("gx", "gy")
     return jax.shard_map(

time: 32.1 us -> 26.8 us (0.83)
  Pallas kernels: 29.1 us -> 26 us
  local copies, waits for them, and re-layouts: 2.14 us -> 0 us
    pallas_call x1, Pallas kernels: 29.1 us -> 25.3 us  [per_device(): pl.pallas_call(functools.partial(kernel, gy), out_shape=[jax.ShapeDtypeSt...]
    unnamed x4 -> x0, local copies, waits for them, and re-layouts: 2.14 us -> none
    pallas_call x0 -> x1, Pallas kernels: none -> 0.67 us  [per_device(): pl.pallas_call(write, out_shape=[jax.ShapeDtypeStruct((64, 256), F32)] *...]
where the time goes in v3:
time: 26.8 us; the launch traced here: 26.7 us
  Pallas kernels  26 us (97%)
  between operations  0.64 us (2%)
    pallas_call x1, Pallas kernels, per_device(): pl.pallas_call(functools.partial(kernel, gy), out_shape=[jax.ShapeDtypeSt...  25.3 us
    pallas_call x1, Pallas kernels, per_device(): pl.pallas_call(write, out_shape=[jax.ShapeDtypeStruct((64, 256), F32)] *...  0.67 us

profile of v3, /device:TPU:1, one launch (start us, length us, event | category | flops | bytes accessed | tf_op | source)
XLA Modules:
  0.0 26.7 jit_solution(10946601187644586872)
XLA Ops:
  0.6 25.3 %shard_map.68 = (f32[64,256]{1,0:T(8,128)S(1)}, f32[64,256]{1,0:T(8,128)S(1)}) custom-call(f32[64,256]{1,0:T(8,128)} %refs_0_.1, f32[64,256]{1,0:T(8,128)} %refs_1_.1, f32[64,256]{1,0:T(8,128)} %refs_2_.1, f32[64,256]{1,0:T(8,128)} %refs_3_.1, f32[64,256]{1,0:T(8,128)} %refs_4_.1), custom_call_target="tpu_custom_call" | custom-call | tf_op jit(solution)/shard_map/pallas_call | solution.py:352
  26.0 0.7 %shard_map.69 = (f32[64,256]{1,0:T(8,128)}, f32[64,256]{1,0:T(8,128)}) custom-call(f32[64,256]{1,0:T(8,128)S(1)} %get-tuple-element.4.refs_0_, f32[64,256]{1,0:T(8,128)S(1)} %get-tuple-element.5.refs_1_), custom_call_target="tpu_custom_call" | custom-call | tf_op jit(solution)/shard_map/pallas_call | solution.py:383

commit v4 on v3

--- a/solution.py
+++ b/solution.py
@@ -146,15 +146,18 @@
         if rows == 128 - CHUNK:
             ref[at + (pl.ds(0, 8),)] = value[CHUNK - 8 :]
 
-    def operate(slot, tile, rows):
+    def operate(slot, tile, rows, centre):
         here = pl.ds(rows, CHUNK)
-        centre = field[slot, tile, pl.ds(8 + rows, CHUNK)]
-        total = coef[0, here] * centre
-        for number, (offset, _, _) in enumerate(STENCIL):
-            total = total + coef[1 + number, here] * field[slot, tile, pl.ds(8 + rows + offset, CHUNK)]
-        for number, (offset, _, _) in enumerate(STENCIL):
-            total = total + coef[5 + number, here] * pltpu.roll(centre, (-offset) % 128, 1)
-        return centre, total
+        turned = [
+            coef[5 + number, here] * pltpu.roll(centre, (-offset) % 128, 1)
+            for number, (offset, _, _) in enumerate(STENCIL)
+        ]
+        moved = [
+            coef[1 + number, here] * field[slot, tile, pl.ds(8 + rows + offset, CHUNK)]
+            for number, (offset, _, _) in enumerate(STENCIL)
+        ]
+        still = coef[0, here] * centre + ((moved[0] + moved[1]) + (moved[2] + moved[3]))
+        return still, (turned[0] + turned[1]) + (turned[2] + turned[3])
 
     def half(phase, carry):
         tile = lax.rem(1 - c + phase, 2)
@@ -196,22 +199,30 @@
                 other = pltpu.roll(vy, (-offset) % 128, 1)
                 coef[5 + number, here] = flat + slope * (vy + other)
         for rows in ROWS:
-            _, total = operate(0, tile, rows)
-            value = gather(0, rows) - (1.0 / SCALE) * total
+            still, turned = operate(0, tile, rows, field[0, tile, pl.ds(8 + rows, CHUNK)])
+            value = gather(0, rows) - (1.0 / SCALE) * (still + turned)
             put(field, (1, tile), rows, value)
             pltpu.store(image.at[STEPS, pl.ds(rows, CHUNK)], value, mask=core_lanes)
 
-        def step(k, carry):
-            centre_k = table[0, k]
-            link_k = table[1, k]
-            for rows in ROWS:
-                now, total = operate(k + 1, tile, rows)
-                before = field[k, tile, pl.ds(8 + rows, CHUNK)]
-                put(field, (k + 2, tile), rows, total - centre_k * now - link_k * before)
-                pltpu.store(image.at[k, pl.ds(rows, CHUNK)], total, mask=core_lanes)
+        def steps(turn, carry):
+            centres = None
+            for k in [turn * 5 + part for part in range(5)]:
+                centre_k = table[0, k]
+                link_k = table[1, k]
+                afters = []
+                for index, rows in enumerate(ROWS):
+                    now = centres[index] if centres else field[k + 1, tile, pl.ds(8 + rows, CHUNK)]
+                    still, turned = operate(k + 1, tile, rows, now)
+                    before = field[k, tile, pl.ds(8 + rows, CHUNK)]
+                    rest = still - centre_k * now - link_k * before
+                    after = rest + turned
+                    put(field, (k + 2, tile), rows, after)
+                    pltpu.store(image.at[k, pl.ds(rows, CHUNK)], still + turned, mask=core_lanes)
+                    afters.append(after)
+                centres = afters
             return carry
 
-        return lax.fori_loop(0, STEPS, step, carry)
+        return lax.fori_loop(0, STEPS // 5, steps, carry)
 
     lax.fori_loop(0, 2, half, 0)
 

time: 26.8 us -> 26.2 us (0.978)
  Pallas kernels: 26 us -> 25.4 us
    pallas_call x1, Pallas kernels: 25.3 us -> 24.7 us  [per_device(): pl.pallas_call(functools.partial(kernel, gy), out_shape=[jax.ShapeDtypeSt...]
where the time goes in v4:
time: 26.2 us; the launch traced here: 26 us
  Pallas kernels  25.4 us (97%)
  between operations  0.64 us (2%)
    pallas_call x1, Pallas kernels, per_device(): pl.pallas_call(functools.partial(kernel, gy), out_shape=[jax.ShapeDtypeSt...  24.7 us
    pallas_call x1, Pallas kernels, per_device(): pl.pallas_call(write, out_shape=[jax.ShapeDtypeStruct((64, 256), F32)] *...  0.67 us

profile of v4, /device:TPU:1, one launch (start us, length us, event | category | flops | bytes accessed | tf_op | source)
XLA Modules:
  0.0 26.0 jit_solution(8428047135627301893)
XLA Ops:
  0.6 24.7 %shard_map.68 = (f32[64,256]{1,0:T(8,128)S(1)}, f32[64,256]{1,0:T(8,128)S(1)}) custom-call(f32[64,256]{1,0:T(8,128)} %refs_0_.1, f32[64,256]{1,0:T(8,128)} %refs_1_.1, f32[64,256]{1,0:T(8,128)} %refs_2_.1, f32[64,256]{1,0:T(8,128)} %refs_3_.1, f32[64,256]{1,0:T(8,128)} %refs_4_.1), custom_call_target="tpu_custom_call" | custom-call | tf_op jit(solution)/shard_map/pallas_call | solution.py:363
  25.3 0.7 %shard_map.69 = (f32[64,256]{1,0:T(8,128)}, f32[64,256]{1,0:T(8,128)}) custom-call(f32[64,256]{1,0:T(8,128)S(1)} %get-tuple-element.4.refs_0_, f32[64,256]{1,0:T(8,128)S(1)} %get-tuple-element.5.refs_1_), custom_call_target="tpu_custom_call" | custom-call | tf_op jit(solution)/shard_map/pallas_call | solution.py:394

commit v5 on v4

--- a/solution.py
+++ b/solution.py
@@ -132,12 +132,17 @@
     lane = lanes((CHUNK, 128))
     ROWS = range(0, 128, CHUNK)
     near = pl.multiple_of(128 - my_cols, 128)
-    part.wait()
-    for q in range(5):
-        for rows in ROWS:
-            here = pl.ds(rows, CHUNK)
-            plain[q, here] = pltpu.roll(buf[q, here, pl.ds(my_cols, 128)], 32, 1)
-            edge[q, here] = pltpu.roll(buf[q, here, pl.ds(near, 128)], 32, 1)
+
+    def turn_in(first):
+        for q in range(5):
+            for rows in range(0, 64, CHUNK):
+                here = pl.ds(pl.multiple_of(first + rows, CHUNK), CHUNK)
+                plain[q, here] = pltpu.roll(buf[q, here, pl.ds(my_cols, 128)], 32, 1)
+                edge[q, here] = pltpu.roll(buf[q, here, pl.ds(near, 128)], 32, 1)
+
+    turn_in(mine)
+    part.wait_recv()
+    turn_in(theirs)
 
     def put(ref, at, rows, value):
         ref[at + (pl.ds(8 + rows, CHUNK),)] = value
@@ -173,9 +178,6 @@
                 for q in range(4):
                     far = halo[side, pl.ds(64, 16)]
                     edge[4, pl.ds(64 * side + 16 * q, 16)] = pltpu.roll(far, 128 - 32 * q, 1) if q else far
-            pl.semaphore_wait(meet.at[0], sizes[2] - 1)
-            for to in line(1):
-                signal(meet.at[1], to)
 
         halo_lanes = (lane >= 32 * tile) & (lane < 32 * tile + 32)
         core_lanes = ((lane >= 32) & (lane < 96)).astype(jnp.int32) == 1 - tile
@@ -224,7 +226,11 @@
 
         return lax.fori_loop(0, STEPS // 5, steps, carry)
 
-    lax.fori_loop(0, 2, half, 0)
+    lax.fori_loop(0, 1, half, 0)
+    pl.semaphore_wait(meet.at[0], sizes[2] - 1)
+    for to in line(1):
+        signal(meet.at[1], to)
+    lax.fori_loop(1, 2, half, 0)
 
     def core(lane, first, second):
         return jnp.where((lane >= 32) & (lane < 96), first, second)
@@ -232,14 +238,14 @@
     for number, (bi, bj) in enumerate(BLOCKS):
 
         def products(row, sums, bi=bi, bj=bj):
-            for part in range(4):
-                at = pl.ds(pl.multiple_of(row * 32 + 8 * part, 8), 8)
+            for part in range(8):
+                at = pl.ds(pl.multiple_of(row * 64 + 8 * part, 8), 8)
                 left = [image[4 * bi + a, at] for a in range(4)]
                 right = left if bi == bj else [image[4 * bj + b, at] for b in range(4)]
                 sums = tuple(sums[4 * a + b] + left[a] * right[b] for a in range(4) for b in range(4))
             return sums
 
-        sums = lax.fori_loop(0, 4, products, (jnp.zeros((8, 128), F32),) * 16)
+        sums = lax.fori_loop(0, 2, products, (jnp.zeros((8, 128), F32),) * 16)
         for a in range(16):
             acc[number * 16 + a] = sums[a]
 
@@ -332,6 +338,7 @@
         outs[o][:, pl.ds(my_cols, 128)] = done[o, pl.ds(mine, 64)]
     for away in aways:
         away.wait()
+    part.wait_send()
     for edge_copy in edges:
         edge_copy.wait_send()
     pltpu.make_async_copy(others, others, sum_sem.at[0]).wait()

time: 26.2 us -> 26 us (level)
  no operation moved by 1% of the time
where the time goes in v5:
time: 26 us; the launch traced here: 25.8 us
  Pallas kernels  25.2 us (97%)
  between operations  0.64 us (2%)
    pallas_call x1, Pallas kernels, per_device(): pl.pallas_call(functools.partial(kernel, gy), out_shape=[jax.ShapeDtypeSt...  24.5 us
    pallas_call x1, Pallas kernels, per_device(): pl.pallas_call(write, out_shape=[jax.ShapeDtypeStruct((64, 256), F32)] *...  0.67 us

profile of v5, /device:TPU:1, one launch (start us, length us, event | category | flops | bytes accessed | tf_op | source)
XLA Modules:
  0.0 25.8 jit_solution(9055261733176378946)
XLA Ops:
  0.6 24.5 %shard_map.68 = (f32[64,256]{1,0:T(8,128)S(1)}, f32[64,256]{1,0:T(8,128)S(1)}) custom-call(f32[64,256]{1,0:T(8,128)} %refs_0_.1, f32[64,256]{1,0:T(8,128)} %refs_1_.1, f32[64,256]{1,0:T(8,128)} %refs_2_.1, f32[64,256]{1,0:T(8,128)} %refs_3_.1, f32[64,256]{1,0:T(8,128)} %refs_4_.1), custom_call_target="tpu_custom_call" | custom-call | tf_op jit(solution)/shard_map/pallas_call | solution.py:370
  25.2 0.7 %shard_map.69 = (f32[64,256]{1,0:T(8,128)}, f32[64,256]{1,0:T(8,128)}) custom-call(f32[64,256]{1,0:T(8,128)S(1)} %get-tuple-element.4.refs_0_, f32[64,256]{1,0:T(8,128)S(1)} %get-tuple-element.5.refs_1_), custom_call_target="tpu_custom_call" | custom-call | tf_op jit(solution)/shard_map/pallas_call | solution.py:401

commit v6 on v5

--- a/solution.py
+++ b/solution.py
@@ -242,14 +242,21 @@
                 at = pl.ds(pl.multiple_of(row * 64 + 8 * part, 8), 8)
                 left = [image[4 * bi + a, at] for a in range(4)]
                 right = left if bi == bj else [image[4 * bj + b, at] for b in range(4)]
-                sums = tuple(sums[4 * a + b] + left[a] * right[b] for a in range(4) for b in range(4))
+                sums = tuple(
+                    sums[4 * a + b] if bi == bj and a > b else sums[4 * a + b] + left[a] * right[b]
+                    for a in range(4)
+                    for b in range(4)
+                )
             return sums
 
         sums = lax.fori_loop(0, 2, products, (jnp.zeros((8, 128), F32),) * 16)
         for a in range(16):
-            acc[number * 16 + a] = sums[a]
-
-    totals = jnp.sum(jnp.sum(acc[...], axis=1), axis=1, keepdims=True)
+            acc[pl.ds(number * 128 + 8 * a, 8)] = sums[a]
+
+    folded = [acc[pl.ds(part, 160, stride=8)] for part in range(8)]
+    while len(folded) > 1:
+        folded = [one + other for one, other in zip(folded[::2], folded[1::2])]
+    totals = jnp.sum(folded[0], axis=1, keepdims=True)
     wide = jnp.broadcast_to(totals[:128], (128, 128))
     pick = lax.broadcasted_iota(jnp.int32, (128, 128), 0) == lanes((128, 128))
     msg[pl.ds(0, 1)] = jnp.sum(jnp.where(pick, wide, 0.0), axis=0, keepdims=True)
@@ -382,7 +389,7 @@
                 pltpu.VMEM((9, 128, 128), F32),
                 pltpu.VMEM((STEPS + 2, 2, 144, 128), F32),
                 pltpu.VMEM((STEPS + 1, 128, 128), F32),
-                pltpu.VMEM((160, 8, 128), F32),
+                pltpu.VMEM((1280, 128), F32),
                 pltpu.VMEM((2, 128), F32),
                 pltpu.VMEM((n, 2, 128), F32),
                 pltpu.VMEM((160, 128), F32),

time: 26 us -> 25.9 us (level)
  no operation moved by 1% of the time
where the time goes in v6:
time: 25.9 us; the launch traced here: 25.8 us
  Pallas kernels  25.1 us (97%)
  between operations  0.64 us (2%)
    pallas_call x1, Pallas kernels, per_device(): pl.pallas_call(functools.partial(kernel, gy), out_shape=[jax.ShapeDtypeSt...  24.5 us
    pallas_call x1, Pallas kernels, per_device(): pl.pallas_call(write, out_shape=[jax.ShapeDtypeStruct((64, 256), F32)] *...  0.67 us

profile of v6, /device:TPU:1, one launch (start us, length us, event | category | flops | bytes accessed | tf_op | source)
XLA Modules:
  0.0 25.8 jit_solution(1055412213966667908)
XLA Ops:
  0.6 24.5 %shard_map.68 = (f32[64,256]{1,0:T(8,128)S(1)}, f32[64,256]{1,0:T(8,128)S(1)}) custom-call(f32[64,256]{1,0:T(8,128)} %refs_0_.1, f32[64,256]{1,0:T(8,128)} %refs_1_.1, f32[64,256]{1,0:T(8,128)} %refs_2_.1, f32[64,256]{1,0:T(8,128)} %refs_3_.1, f32[64,256]{1,0:T(8,128)} %refs_4_.1), custom_call_target="tpu_custom_call" | custom-call | tf_op jit(solution)/shard_map/pallas_call | solution.py:377
  25.1 0.7 %shard_map.69 = (f32[64,256]{1,0:T(8,128)}, f32[64,256]{1,0:T(8,128)}) custom-call(f32[64,256]{1,0:T(8,128)S(1)} %get-tuple-element.4.refs_0_, f32[64,256]{1,0:T(8,128)S(1)} %get-tuple-element.5.refs_1_), custom_call_target="tpu_custom_call" | custom-call | tf_op jit(solution)/shard_map/pallas_call | solution.py:408

commit v7 on v6

--- a/solution.py
+++ b/solution.py
@@ -306,7 +306,7 @@
     weights = [None] * STEPS
     for k in reversed(range(STEPS)):
         value = goal[k]
-        for i in range(k + 1, STEPS):
+        for i in reversed(range(k + 1, STEPS)):
             value = value - gram[i][k] * weights[i]
         weights[k] = value * inverse[k]
 

time: 25.9 us -> 25.8 us (level)
  no operation moved by 1% of the time
where the time goes in v7:
time: 25.8 us; the launch traced here: 25.7 us
  Pallas kernels  25 us (97%)
  between operations  0.64 us (2%)
    pallas_call x1, Pallas kernels, per_device(): pl.pallas_call(functools.partial(kernel, gy), out_shape=[jax.ShapeDtypeSt...  24.4 us
    pallas_call x1, Pallas kernels, per_device(): pl.pallas_call(write, out_shape=[jax.ShapeDtypeStruct((64, 256), F32)] *...  0.67 us

profile of v7, /device:TPU:1, one launch (start us, length us, event | category | flops | bytes accessed | tf_op | source)
XLA Modules:
  0.0 25.7 jit_solution(12980899094087616198)
XLA Ops:
  0.6 24.4 %shard_map.68 = (f32[64,256]{1,0:T(8,128)S(1)}, f32[64,256]{1,0:T(8,128)S(1)}) custom-call(f32[64,256]{1,0:T(8,128)} %refs_0_.1, f32[64,256]{1,0:T(8,128)} %refs_1_.1, f32[64,256]{1,0:T(8,128)} %refs_2_.1, f32[64,256]{1,0:T(8,128)} %refs_3_.1, f32[64,256]{1,0:T(8,128)} %refs_4_.1), custom_call_target="tpu_custom_call" | custom-call | tf_op jit(solution)/shard_map/pallas_call | solution.py:377
  25.0 0.7 %shard_map.69 = (f32[64,256]{1,0:T(8,128)}, f32[64,256]{1,0:T(8,128)}) custom-call(f32[64,256]{1,0:T(8,128)S(1)} %get-tuple-element.4.refs_0_, f32[64,256]{1,0:T(8,128)S(1)} %get-tuple-element.5.refs_1_), custom_call_target="tpu_custom_call" | custom-call | tf_op jit(solution)/shard_map/pallas_call | solution.py:408
